TPU v7x, 512 devices: a whole 4x8x8 slice. The times are simulated.
512 devices in a mesh: rows: 128 (over x_hi, z, y), feat: 4 (over x_lo, core).
Axes of the slice: x: 4 (x_hi: 2, x_lo: 2; x = x_hi * 2 + x_lo), y: 8, z: 8, core: 2. Of those that a mesh axis runs over, the one named last changes fastest.
Arguments:
- features: bfloat16 [131072, 64], P('rows', 'feat'), may hold values from -0.75 to 0.75
- probes: bfloat16 [131072, 32], P('rows', 'feat'), may hold values from -6 to 6
- theta: float32 [1], replicated, may hold values from 0.18 to 0.69
- block_mask: int32 [128, 9], P('rows'), may hold values 0 or 1
- order: int32 [128, 1024], P('rows'), may hold values from 0 to 1023, each once within a row
Outputs:
- kernel_probes: float32 [131072, 32], P('rows', 'feat')
- deriv_probes: float32 [131072, 32], P('rows', 'feat')
All inputs are finite; a program needn't handle non-finite values. No bound on the sum of `block_mask` on one device may be relied on, other than what follows from the above.
Results may differ from a plain program's by a relative error of at most 0.003.
Values may be sent and summed in bfloat16 or wider, within the bound.
A program may use at most 64 MiB of HBM per device.

v0:
```python
import jax
import jax.numpy as jnp
from jax import lax
from jax.sharding import PartitionSpec as P


def sent_to_all(value, axis):
    copies = jnp.broadcast_to(value, (lax.axis_size(axis), *value.shape))
    return lax.all_to_all(copies, axis, split_axis=0, concat_axis=0, tiled=True)


def in_order(tiles, dim):
    shape = list(tiles.shape[1:])
    shape[dim] *= tiles.shape[0]
    return jnp.moveaxis(tiles, 0, dim).reshape(shape)


def collect(value, axis, dim):
    tiles = sent_to_all(value, axis)
    return in_order(tiles, dim)


def passed_along(value, axis, steps):
    count = lax.axis_size(axis)
    pairs = [(source, (source + steps) % count) for source in range(count)]
    return lax.ppermute(value, axis, pairs)


def split_up(value, dim, devices):
    shape = value.shape
    tiles = value.reshape(*shape[:dim], devices, shape[dim] // devices, *shape[dim + 1 :])
    return jnp.moveaxis(tiles, dim, 0)


def sent_and_summed(value, axis, dim):
    tiles = split_up(value, dim, lax.axis_size(axis))
    arrived = lax.all_to_all(tiles, axis, split_axis=0, concat_axis=0, tiled=True)
    return arrived.sum(axis=0)


def sent_together(arrays, axis, dim, along):
    widths = [a.shape[along] for a in arrays]
    both = jnp.concatenate(arrays, axis=along)
    out = sent_and_summed(both, axis, dim)
    return tuple(jnp.split(out, [sum(widths[:k]) for k in range(1, len(widths))], axis=along))


def body(features, probes, theta, block_mask, order):
    own_full = lax.all_gather(features, "feat", axis=1, tiled=True)
    scale = jnp.exp(-2.0 * theta[0])
    own_sq = jnp.sum(own_full.astype(jnp.float32) ** 2, axis=1)
    rows_here = probes.shape[0]

    def tile_terms(panel_full, panel_probes, active):
        panel_sq = jnp.sum(panel_full.astype(jnp.float32) ** 2, axis=1)
        cross = lax.dot_general(
            own_full, panel_full, (((1,), (1,)), ((), ())), preferred_element_type=jnp.float32
        )
        dist2 = jnp.maximum(own_sq[:, None] + panel_sq[None, :] - 2.0 * cross, 0.0)
        radius2 = dist2 * scale
        radius = jnp.sqrt(radius2)
        inside = jnp.maximum(1.0 - radius, 0.0)
        inside2 = inside * inside
        kern = (inside2 * inside2 * (4.0 * radius + 1.0)).astype(jnp.bfloat16)
        deriv = (20.0 * radius2 * inside2 * inside).astype(jnp.bfloat16)
        first = jnp.dot(kern, panel_probes, preferred_element_type=jnp.float32)
        second = jnp.dot(deriv, panel_probes, preferred_element_type=jnp.float32)
        weight = (active > 0).astype(jnp.float32)
        return (first * weight, second * weight)

    all_probes = collect(probes, "feat", 1)
    ordered_all = jnp.take(all_probes, order[0], axis=0)
    quarter = rows_here // lax.axis_size("feat")
    start = lax.axis_index("feat") * quarter
    carried = lax.dynamic_slice_in_dim(own_full, start, quarter, 0)
    panel_probes = lax.dynamic_slice_in_dim(ordered_all, start, quarter, 0)
    total_k, total_d = tile_terms(carried, panel_probes, jnp.int32(1))
    upper = (carried, panel_probes)
    lower = (carried, panel_probes)
    for step in range(1, 5):
        upper = passed_along((upper[0], upper[1]), "rows", -1)
        lower = passed_along((lower[0], lower[1]), "rows", 1)
        add_k, add_d = tile_terms(upper[0], upper[1], block_mask[0, 4 + step])
        total_k, total_d = (total_k + add_k, total_d + add_d)
        add_k, add_d = tile_terms(lower[0], lower[1], block_mask[0, 4 - step])
        total_k, total_d = (total_k + add_k, total_d + add_d)
    total_k, total_d = sent_together((total_k, total_d), "feat", 1, 0)
    return (total_k, total_d)


def solution(mesh):
    return jax.shard_map(
        body,
        mesh=mesh,
        in_specs=(P("rows", "feat"), P("rows", "feat"), P(), P("rows", None), P("rows", None)),
        out_specs=(P("rows", "feat"), P("rows", "feat")),
        check_vma=False,
    )
```

profile of v0, /device:TPU:1, one launch (start us, length us, event | category | flops | bytes accessed | tf_op | source)
XLA Modules:
  0.0 137.9 jit_solution(5949143357094899956)
XLA Ops:
  0.6 12.3 %all_gather.3 = bf16[1024,64]{0,1:T(8,128)(2,1)S(1)} all-gather(bf16[1024,16]{0,1:T(8,128)(2,1)} %param.5), channel_id=1, replica_groups=mesh['rows'=128,'feat'=4] {'feat'}, dimensions={1}, use_global_device_ids=true | all-gather | bytes 163840 | tf_op jit(solution)/shard_map/all_gather | solution.py:49
  13.0 10.7 %collective-permute-start = (bf16[256,64]{0,1:T(8,128)(2,1)S(1)}, bf16[256,64]{0,1:T(8,128)(2,1)S(1)}, u32[]{:S(2)}, u32[]{:S(2)}) collective-permute-start(bf16[256,64]{0,1:T(8,128)(2,1)S(1)} %get-tuple-element.3), channel_id=1, source_target_pairs={{0,508},{4,0},{8,4},{12,8},{16,12},{20,16},{24,20},{28,24},{32,28}... | collective-permute-start | bytes 98312 | tf_op jit(solution)/shard_map/ppermute | solution.py:26
  23.7 1.9 %collective-permute-start.2 = (bf16[256,64]{0,1:T(8,128)(2,1)S(1)}, bf16[256,64]{0,1:T(8,128)(2,1)S(1)}, u32[]{:S(2)}, u32[]{:S(2)}) collective-permute-start(bf16[256,64]{0,1:T(8,128)(2,1)S(1)} %get-tuple-element.3), channel_id=1, source_target_pairs={{0,4},{4,8},{8,12},{12,16},{16,20},{20,24},{24,28},{28,32},{32,36}... | collective-permute-start | bytes 98312 | tf_op jit(solution)/shard_map/ppermute | solution.py:26
  26.2 3.7 %all-to-all-start = ((bf16[4,1024,8]{1,2,0:T(8,128)(2,1)}), bf16[4,1024,8]{1,2,0:T(8,128)(2,1)S(1)}, u32[]{:S(2)}, u32[]{:S(2)}) async-start(bf16[4,1024,8]{1,2,0:T(8,128)(2,1)} %broadcast_in_dim.13), calls=%async_computation | async-start | bytes 131072 | tf_op jit(solution)/shard_map/all_to_all | solution.py:9
  30.7 1.3 fusion.11
  37.9 9.4 %collective-permute-start.4 = (bf16[256,64]{0,1:T(8,128)(2,1)S(1)}, bf16[256,64]{0,1:T(8,128)(2,1)S(1)}, u32[]{:S(2)}, u32[]{:S(2)}) collective-permute-start(bf16[256,64]{0,1:T(8,128)(2,1)S(1)} %collective-permute-done), channel_id=1, source_target_pairs={{0,508},{4,0},{8,4},{12,8},{16,12},{20,16},{24,20},{28,24},{32,28}... | collective-permute-start | bytes 98312 | tf_op jit(solution)/shard_map/ppermute | solution.py:26
  47.3 1.9 %collective-permute-start.6 = (bf16[256,64]{0,1:T(8,128)(2,1)S(1)}, bf16[256,64]{0,1:T(8,128)(2,1)S(1)}, u32[]{:S(2)}, u32[]{:S(2)}) collective-permute-start(bf16[256,64]{0,1:T(8,128)(2,1)S(1)} %collective-permute-done.2), channel_id=1, source_target_pairs={{0,4},{4,8},{8,12},{12,16},{16,20},{20,24},{24,28},{28,32},{32,36}... | collective-permute-start | bytes 98312 | tf_op jit(solution)/shard_map/ppermute | solution.py:26
  50.1 3.2 %gather_fusion = bf16[1024,32]{1,0:T(8,128)(2,1)S(1)} fusion(bf16[1024,32]{1,0:T(8,128)(2,1)S(1)} %copy.8, s32[1024]{0:T(1024)S(1)} %broadcast_clamp_fusion), kind=kCustom, calls=%fused_computation | custom fusion | bytes 135168 | tf_op jit(solution)/shard_map/jit(_take)/gather | solution.py:72
  53.4 2.1 %collective-permute-start.3 = (bf16[256,32]{1,0:T(8,128)(2,1)S(1)}, bf16[256,32]{1,0:T(8,128)(2,1)S(1)}, u32[]{:S(2)}, u32[]{:S(2)}) collective-permute-start(bf16[256,32]{1,0:T(8,128)(2,1)S(1)} %dynamic-slice_select_fusion), channel_id=1, source_target_pairs={{0,4},{4,8},{8,12},{12,16},{16,20},{20,24},{24,28},{28,32},{32,36}... | collective-permute-start | bytes 49160 | tf_op jit(solution)/shard_map/ppermute | solution.py:26
  55.5 9.1 %collective-permute-start.1 = (bf16[256,32]{1,0:T(8,128)(2,1)S(1)}, bf16[256,32]{1,0:T(8,128)(2,1)S(1)}, u32[]{:S(2)}, u32[]{:S(2)}) collective-permute-start(bf16[256,32]{1,0:T(8,128)(2,1)S(1)} %dynamic-slice_select_fusion), channel_id=1, source_target_pairs={{0,508},{4,0},{8,4},{12,8},{16,12},{20,16},{24,20},{28,24},{32,28}... | collective-permute-start | bytes 49160 | tf_op jit(solution)/shard_map/ppermute | solution.py:26
  64.5 1.8 %fusion.28 = f32[1024,32]{0,1:T(8,128)S(1)} fusion(bf16[256,32]{1,0:T(8,128)(2,1)S(1)} %dynamic-slice_select_fusion, f32[1024,256]{0,1:T(8,128)} %fusion.11), kind=kOutput, calls=%fused_computation.89 | convolution fusion | flops 18612224 | bytes 1196032 | tf_op jit(solution)/shard_map/dot_general | solution.py:67
  67.0 3.4 %collective-permute-start.8 = (bf16[256,64]{0,1:T(8,128)(2,1)S(1)}, bf16[256,64]{0,1:T(8,128)(2,1)S(1)}, u32[]{:S(2)}, u32[]{:S(2)}) collective-permute-start(bf16[256,64]{0,1:T(8,128)(2,1)S(1)} %collective-permute-done.4), channel_id=1, source_target_pairs={{0,508},{4,0},{8,4},{12,8},{16,12},{20,16},{24,20},{28,24},{32,28}... | collective-permute-start | bytes 98312 | tf_op jit(solution)/shard_map/ppermute | solution.py:26
  70.4 1.9 %collective-permute-start.10 = (bf16[256,64]{0,1:T(8,128)(2,1)S(1)}, bf16[256,64]{0,1:T(8,128)(2,1)S(1)}, u32[]{:S(2)}, u32[]{:S(2)}) collective-permute-start(bf16[256,64]{0,1:T(8,128)(2,1)S(1)} %collective-permute-done.6), channel_id=1, source_target_pairs={{0,4},{4,8},{8,12},{12,16},{16,20},{20,24},{24,28},{28,32},{32,36}... | collective-permute-start | bytes 98312 | tf_op jit(solution)/shard_map/ppermute | solution.py:26
  73.0 1.9 %collective-permute-start.7 = (bf16[256,32]{1,0:T(8,128)(2,1)S(1)}, bf16[256,32]{1,0:T(8,128)(2,1)S(1)}, u32[]{:S(2)}, u32[]{:S(2)}) collective-permute-start(bf16[256,32]{1,0:T(8,128)(2,1)S(1)} %collective-permute-done.3), channel_id=1, source_target_pairs={{0,4},{4,8},{8,12},{12,16},{16,20},{20,24},{24,28},{28,32},{32,36}... | collective-permute-start | bytes 49160 | tf_op jit(solution)/shard_map/ppermute | solution.py:26
  74.9 9.1 %collective-permute-start.5 = (bf16[256,32]{1,0:T(8,128)(2,1)S(1)}, bf16[256,32]{1,0:T(8,128)(2,1)S(1)}, u32[]{:S(2)}, u32[]{:S(2)}) collective-permute-start(bf16[256,32]{1,0:T(8,128)(2,1)S(1)} %collective-permute-done.1), channel_id=1, source_target_pairs={{0,508},{4,0},{8,4},{12,8},{16,12},{20,16},{24,20},{28,24},{32,28}... | collective-permute-start | bytes 49160 | tf_op jit(solution)/shard_map/ppermute | solution.py:26
  84.8 0.8 fusion.27
  87.3 1.9 %collective-permute-start.11 = (bf16[256,32]{1,0:T(8,128)(2,1)S(1)}, bf16[256,32]{1,0:T(8,128)(2,1)S(1)}, u32[]{:S(2)}, u32[]{:S(2)}) collective-permute-start(bf16[256,32]{1,0:T(8,128)(2,1)S(1)} %collective-permute-done.7), channel_id=1, source_target_pairs={{0,4},{4,8},{8,12},{12,16},{16,20},{20,24},{24,28},{28,32},{32,36}... | collective-permute-start | bytes 49160 | tf_op jit(solution)/shard_map/ppermute | solution.py:26
  90.9 9.1 %collective-permute-start.9 = (bf16[256,32]{1,0:T(8,128)(2,1)S(1)}, bf16[256,32]{1,0:T(8,128)(2,1)S(1)}, u32[]{:S(2)}, u32[]{:S(2)}) collective-permute-start(bf16[256,32]{1,0:T(8,128)(2,1)S(1)} %collective-permute-done.5), channel_id=1, source_target_pairs={{0,508},{4,0},{8,4},{12,8},{16,12},{20,16},{24,20},{28,24},{32,28}... | collective-permute-start | bytes 49160 | tf_op jit(solution)/shard_map/ppermute | solution.py:26
  101.7 1.9 %collective-permute-start.12 = (bf16[256,64]{0,1:T(8,128)(2,1)S(1)}, bf16[256,64]{0,1:T(8,128)(2,1)S(1)}, u32[]{:S(2)}, u32[]{:S(2)}) collective-permute-start(bf16[256,64]{0,1:T(8,128)(2,1)S(1)} %collective-permute-done.8), channel_id=1, source_target_pairs={{0,508},{4,0},{8,4},{12,8},{16,12},{20,16},{24,20},{28,24},{32,28}... | collective-permute-start | bytes 98312 | tf_op jit(solution)/shard_map/ppermute | solution.py:26
  103.6 3.4 %collective-permute-start.14 = (bf16[256,64]{0,1:T(8,128)(2,1)S(1)}, bf16[256,64]{0,1:T(8,128)(2,1)S(1)}, u32[]{:S(2)}, u32[]{:S(2)}) collective-permute-start(bf16[256,64]{0,1:T(8,128)(2,1)S(1)} %collective-permute-done.10), channel_id=1, source_target_pairs={{0,4},{4,8},{8,12},{12,16},{16,20},{20,24},{24,28},{28,32},{32,36}... | collective-permute-start | bytes 98312 | tf_op jit(solution)/shard_map/ppermute | solution.py:26
  107.7 1.9 %collective-permute-start.15 = (bf16[256,32]{1,0:T(8,128)(2,1)S(1)}, bf16[256,32]{1,0:T(8,128)(2,1)S(1)}, u32[]{:S(2)}, u32[]{:S(2)}) collective-permute-start(bf16[256,32]{1,0:T(8,128)(2,1)S(1)} %collective-permute-done.11), channel_id=1, source_target_pairs={{0,4},{4,8},{8,12},{12,16},{16,20},{20,24},{24,28},{28,32},{32,36}... | collective-permute-start | bytes 49160 | tf_op jit(solution)/shard_map/ppermute | solution.py:26
  111.2 9.3 %collective-permute-start.13 = (bf16[256,32]{1,0:T(8,128)(2,1)S(1)}, bf16[256,32]{1,0:T(8,128)(2,1)S(1)}, u32[]{:S(2)}, u32[]{:S(2)}) collective-permute-start(bf16[256,32]{1,0:T(8,128)(2,1)S(1)} %collective-permute-done.9), channel_id=1, source_target_pairs={{0,508},{4,0},{8,4},{12,8},{16,12},{20,16},{24,20},{28,24},{32,28}... | collective-permute-start | bytes 49160 | tf_op jit(solution)/shard_map/ppermute | solution.py:26
  120.5 0.8 fusion.23
  126.2 11.1 %all_to_all.10 = f32[4,2048,8]{1,2,0:T(8,128)S(1)} all-to-all(f32[4,2048,8]{1,2,0:T(8,128)S(1)} %maximum_bitcast_fusion), channel_id=1, replica_groups=mesh['rows'=128,'feat'=4] {'feat'}, dimensions={0} | all-to-all | bytes 524288 | tf_op jit(solution)/shard_map/all_to_all | solution.py:37
  (69 shorter events, 17.1 us)
Async XLA Ops:
  12.9 12.7 %copy-start.1 = (bf16[1024,8]{0,1:T(8,128)(2,1)S(1)}, bf16[1024,8]{0,1:T(8,128)(2,1)}, u32[]{:S(2)}) copy-start(bf16[1024,8]{0,1:T(8,128)(2,1)} %param.6) | copy-start | bytes 49156
  13.0 24.9 %collective-permute-start = (bf16[256,64]{0,1:T(8,128)(2,1)S(1)}, bf16[256,64]{0,1:T(8,128)(2,1)S(1)}, u32[]{:S(2)}, u32[]{:S(2)}) collective-permute-start(bf16[256,64]{0,1:T(8,128)(2,1)S(1)} %get-tuple-element.3), channel_id=1, source_target_pairs={{0,508},{4,0},{8,4},{12,8},{16,12},{20,16},{24,20},{28,24},{32,28}... | collective-permute-start | bytes 98312 | tf_op jit(solution)/shard_map/ppermute | solution.py:26
  23.7 23.6 %collective-permute-start.2 = (bf16[256,64]{0,1:T(8,128)(2,1)S(1)}, bf16[256,64]{0,1:T(8,128)(2,1)S(1)}, u32[]{:S(2)}, u32[]{:S(2)}) collective-permute-start(bf16[256,64]{0,1:T(8,128)(2,1)S(1)} %get-tuple-element.3), channel_id=1, source_target_pairs={{0,4},{4,8},{8,12},{12,16},{16,20},{20,24},{24,28},{28,32},{32,36}... | collective-permute-start | bytes 98312 | tf_op jit(solution)/shard_map/ppermute | solution.py:26
  26.2 23.6 %all-to-all-start = ((bf16[4,1024,8]{1,2,0:T(8,128)(2,1)}), bf16[4,1024,8]{1,2,0:T(8,128)(2,1)S(1)}, u32[]{:S(2)}, u32[]{:S(2)}) async-start(bf16[4,1024,8]{1,2,0:T(8,128)(2,1)} %broadcast_in_dim.13), calls=%async_computation | async-start | bytes 131072 | tf_op jit(solution)/shard_map/all_to_all | solution.py:9
  30.0 0.7 copy-start.2
  30.7 1.4 copy-start
  37.9 29.1 %collective-permute-start.4 = (bf16[256,64]{0,1:T(8,128)(2,1)S(1)}, bf16[256,64]{0,1:T(8,128)(2,1)S(1)}, u32[]{:S(2)}, u32[]{:S(2)}) collective-permute-start(bf16[256,64]{0,1:T(8,128)(2,1)S(1)} %collective-permute-done), channel_id=1, source_target_pairs={{0,508},{4,0},{8,4},{12,8},{16,12},{20,16},{24,20},{28,24},{32,28}... | collective-permute-start | bytes 98312 | tf_op jit(solution)/shard_map/ppermute | solution.py:26
  47.3 23.1 %collective-permute-start.6 = (bf16[256,64]{0,1:T(8,128)(2,1)S(1)}, bf16[256,64]{0,1:T(8,128)(2,1)S(1)}, u32[]{:S(2)}, u32[]{:S(2)}) collective-permute-start(bf16[256,64]{0,1:T(8,128)(2,1)S(1)} %collective-permute-done.2), channel_id=1, source_target_pairs={{0,4},{4,8},{8,12},{12,16},{16,20},{20,24},{24,28},{28,32},{32,36}... | collective-permute-start | bytes 98312 | tf_op jit(solution)/shard_map/ppermute | solution.py:26
  53.3 13.1 %copy-start.3 = (f32[1024,256]{0,1:T(8,128)S(1)}, f32[1024,256]{0,1:T(8,128)}, u32[]{:S(2)}) copy-start(f32[1024,256]{0,1:T(8,128)} %fusion.11) | copy-start | bytes 3145732
  53.4 19.6 %collective-permute-start.3 = (bf16[256,32]{1,0:T(8,128)(2,1)S(1)}, bf16[256,32]{1,0:T(8,128)(2,1)S(1)}, u32[]{:S(2)}, u32[]{:S(2)}) collective-permute-start(bf16[256,32]{1,0:T(8,128)(2,1)S(1)} %dynamic-slice_select_fusion), channel_id=1, source_target_pairs={{0,4},{4,8},{8,12},{12,16},{16,20},{20,24},{24,28},{28,32},{32,36}... | collective-permute-start | bytes 49160 | tf_op jit(solution)/shard_map/ppermute | solution.py:26
  55.5 19.5 %collective-permute-start.1 = (bf16[256,32]{1,0:T(8,128)(2,1)S(1)}, bf16[256,32]{1,0:T(8,128)(2,1)S(1)}, u32[]{:S(2)}, u32[]{:S(2)}) collective-permute-start(bf16[256,32]{1,0:T(8,128)(2,1)S(1)} %dynamic-slice_select_fusion), channel_id=1, source_target_pairs={{0,508},{4,0},{8,4},{12,8},{16,12},{20,16},{24,20},{28,24},{32,28}... | collective-permute-start | bytes 49160 | tf_op jit(solution)/shard_map/ppermute | solution.py:26
  67.0 34.6 %collective-permute-start.8 = (bf16[256,64]{0,1:T(8,128)(2,1)S(1)}, bf16[256,64]{0,1:T(8,128)(2,1)S(1)}, u32[]{:S(2)}, u32[]{:S(2)}) collective-permute-start(bf16[256,64]{0,1:T(8,128)(2,1)S(1)} %collective-permute-done.4), channel_id=1, source_target_pairs={{0,508},{4,0},{8,4},{12,8},{16,12},{20,16},{24,20},{28,24},{32,28}... | collective-permute-start | bytes 98312 | tf_op jit(solution)/shard_map/ppermute | solution.py:26
  70.4 33.2 %collective-permute-start.10 = (bf16[256,64]{0,1:T(8,128)(2,1)S(1)}, bf16[256,64]{0,1:T(8,128)(2,1)S(1)}, u32[]{:S(2)}, u32[]{:S(2)}) collective-permute-start(bf16[256,64]{0,1:T(8,128)(2,1)S(1)} %collective-permute-done.6), channel_id=1, source_target_pairs={{0,4},{4,8},{8,12},{12,16},{16,20},{20,24},{24,28},{28,32},{32,36}... | collective-permute-start | bytes 98312 | tf_op jit(solution)/shard_map/ppermute | solution.py:26
  73.0 14.3 %collective-permute-start.7 = (bf16[256,32]{1,0:T(8,128)(2,1)S(1)}, bf16[256,32]{1,0:T(8,128)(2,1)S(1)}, u32[]{:S(2)}, u32[]{:S(2)}) collective-permute-start(bf16[256,32]{1,0:T(8,128)(2,1)S(1)} %collective-permute-done.3), channel_id=1, source_target_pairs={{0,4},{4,8},{8,12},{12,16},{16,20},{20,24},{24,28},{28,32},{32,36}... | collective-permute-start | bytes 49160 | tf_op jit(solution)/shard_map/ppermute | solution.py:26
  74.9 16.0 %collective-permute-start.5 = (bf16[256,32]{1,0:T(8,128)(2,1)S(1)}, bf16[256,32]{1,0:T(8,128)(2,1)S(1)}, u32[]{:S(2)}, u32[]{:S(2)}) collective-permute-start(bf16[256,32]{1,0:T(8,128)(2,1)S(1)} %collective-permute-done.1), channel_id=1, source_target_pairs={{0,508},{4,0},{8,4},{12,8},{16,12},{20,16},{24,20},{28,24},{32,28}... | collective-permute-start | bytes 49160 | tf_op jit(solution)/shard_map/ppermute | solution.py:26
  87.3 20.3 %collective-permute-start.11 = (bf16[256,32]{1,0:T(8,128)(2,1)S(1)}, bf16[256,32]{1,0:T(8,128)(2,1)S(1)}, u32[]{:S(2)}, u32[]{:S(2)}) collective-permute-start(bf16[256,32]{1,0:T(8,128)(2,1)S(1)} %collective-permute-done.7), channel_id=1, source_target_pairs={{0,4},{4,8},{8,12},{12,16},{16,20},{20,24},{24,28},{28,32},{32,36}... | collective-permute-start | bytes 49160 | tf_op jit(solution)/shard_map/ppermute | solution.py:26
  90.9 20.3 %collective-permute-start.9 = (bf16[256,32]{1,0:T(8,128)(2,1)S(1)}, bf16[256,32]{1,0:T(8,128)(2,1)S(1)}, u32[]{:S(2)}, u32[]{:S(2)}) collective-permute-start(bf16[256,32]{1,0:T(8,128)(2,1)S(1)} %collective-permute-done.5), channel_id=1, source_target_pairs={{0,508},{4,0},{8,4},{12,8},{16,12},{20,16},{24,20},{28,24},{32,28}... | collective-permute-start | bytes 49160 | tf_op jit(solution)/shard_map/ppermute | solution.py:26
  101.7 22.5 %collective-permute-start.12 = (bf16[256,64]{0,1:T(8,128)(2,1)S(1)}, bf16[256,64]{0,1:T(8,128)(2,1)S(1)}, u32[]{:S(2)}, u32[]{:S(2)}) collective-permute-start(bf16[256,64]{0,1:T(8,128)(2,1)S(1)} %collective-permute-done.8), channel_id=1, source_target_pairs={{0,508},{4,0},{8,4},{12,8},{16,12},{20,16},{24,20},{28,24},{32,28}... | collective-permute-start | bytes 98312 | tf_op jit(solution)/shard_map/ppermute | solution.py:26
  103.6 18.5 %collective-permute-start.14 = (bf16[256,64]{0,1:T(8,128)(2,1)S(1)}, bf16[256,64]{0,1:T(8,128)(2,1)S(1)}, u32[]{:S(2)}, u32[]{:S(2)}) collective-permute-start(bf16[256,64]{0,1:T(8,128)(2,1)S(1)} %collective-permute-done.10), channel_id=1, source_target_pairs={{0,4},{4,8},{8,12},{12,16},{16,20},{20,24},{24,28},{28,32},{32,36}... | collective-permute-start | bytes 98312 | tf_op jit(solution)/shard_map/ppermute | solution.py:26
  107.7 14.8 %collective-permute-start.15 = (bf16[256,32]{1,0:T(8,128)(2,1)S(1)}, bf16[256,32]{1,0:T(8,128)(2,1)S(1)}, u32[]{:S(2)}, u32[]{:S(2)}) collective-permute-start(bf16[256,32]{1,0:T(8,128)(2,1)S(1)} %collective-permute-done.11), channel_id=1, source_target_pairs={{0,4},{4,8},{8,12},{12,16},{16,20},{20,24},{24,28},{28,32},{32,36}... | collective-permute-start | bytes 49160 | tf_op jit(solution)/shard_map/ppermute | solution.py:26
  111.2 13.3 %collective-permute-start.13 = (bf16[256,32]{1,0:T(8,128)(2,1)S(1)}, bf16[256,32]{1,0:T(8,128)(2,1)S(1)}, u32[]{:S(2)}, u32[]{:S(2)}) collective-permute-start(bf16[256,32]{1,0:T(8,128)(2,1)S(1)} %collective-permute-done.9), channel_id=1, source_target_pairs={{0,508},{4,0},{8,4},{12,8},{16,12},{20,16},{24,20},{28,24},{32,28}... | collective-permute-start | bytes 49160 | tf_op jit(solution)/shard_map/ppermute | solution.py:26
where the time goes:
time: 139 us; the launch traced here: 138 us
  starting transfers between devices  82.5 us (59%)
  blocking collectives  23.4 us (17%)
  matrix products  19.2 us (14%)
  between operations  6.92 us (5%)
  local copies, waits for them, and re-layouts  5.4 us (4%)
    ppermute x16, starting transfers between devices, passed_along(): return lax.ppermute(value, axis, pairs)  78.8 us
    all_gather x1, blocking collectives, body(): own_full = lax.all_gather(features, 'feat', axis=1, tiled=True)  12.3 us
    all_to_all x1, blocking collectives, sent_and_summed(): lax.all_to_all(tiles, axis, split_axis=0, concat_axis=0, tiled=True)  11.1 us
    dot_general x9, matrix products, tile_terms(): second = jnp.dot(deriv, panel_probes, preferred_element_type=jnp.float32)  8.17 us
    dot_general x9, matrix products, tile_terms(): first = jnp.dot(kern, panel_probes, preferred_element_type=jnp.float32)  7.21 us
    dot_general x9, matrix products, tile_terms(): lax.dot_general(own_full, panel_full, (((1,), (1,)), ((), ())), preferred...  3.86 us
    all_to_all x1, starting transfers between devices, sent_to_all(): return lax.all_to_all(copies, axis, split_axis=0, concat_axis=0, tiled=True)  3.69 us
    gather x1, local copies, waits for them, and re-layouts, body(): ordered_all = jnp.take(all_probes, order[0], axis=0)  3.21 us
  transfers between devices with their start and end apart: 17, of which 0 were waited for; matrix products, arithmetic and copies ran while one was open for 16% of the time, Pallas kernels for 0%

commit v1 on v0

--- a/solution.py
+++ b/solution.py
@@ -46,7 +46,9 @@
 
 
 def body(features, probes, theta, block_mask, order):
-    own_full = lax.all_gather(features, "feat", axis=1, tiled=True)
+    own_full = jnp.concatenate(
+        lax.all_to_all(jnp.stack([features] * lax.axis_size("feat")), "feat", 0, 0), axis=1
+    )
     scale = jnp.exp(-2.0 * theta[0])
     own_sq = jnp.sum(own_full.astype(jnp.float32) ** 2, axis=1)
     rows_here = probes.shape[0]

time: 139 us -> 144 us (1.036)
  blocking collectives: 23.4 us -> 12.6 us
  starting transfers between devices: 82.5 us -> 91.7 us
  waiting for transfers between devices: 0.04 us -> 7.53 us
  matrix products: 19.2 us -> 17.1 us
    all_gather x1 -> x0, blocking collectives: 12.3 us -> none  [body(): own_full = lax.all_gather(features, 'feat', axis=1, tiled=True)]
    all_to_all x1, starting transfers between devices: 3.69 us -> 10.2 us  [sent_to_all(): return lax.all_to_all(copies, axis, split_axis=0, concat_axis=0, tiled=True)]
    all_to_all x0 -> x1, starting transfers between devices: none -> 4.57 us  [body(): lax.all_to_all(jnp.stack([features] * lax.axis_size('feat')), 'feat', 0, 0)]
    ppermute x16, waiting for transfers between devices: 0.04 us -> 4.39 us  [passed_along(): return lax.ppermute(value, axis, pairs)]
    all_to_all x1, waiting for transfers between devices: 0.01 us -> 3.14 us  [sent_to_all(): return lax.all_to_all(copies, axis, split_axis=0, concat_axis=0, tiled=True)]
    ppermute x16, starting transfers between devices: 78.8 us -> 76.9 us  [passed_along(): return lax.ppermute(value, axis, pairs)]
    all_to_all x1, blocking collectives: 11.1 us -> 12.6 us  [sent_and_summed(): lax.all_to_all(tiles, axis, split_axis=0, concat_axis=0, tiled=True)]
  transfers between devices with their start and end apart: 17 -> 18, of which waited for: 0 -> 2; matrix products, arithmetic and copies ran while one was open for 16% -> 12% of each run, Pallas kernels for 0% -> 0%
where the time goes in v1:
time: 144 us; the launch traced here: 143 us
  starting transfers between devices  91.7 us (64%)
  matrix products  17.1 us (12%)
  blocking collectives  12.6 us (9%)
  waiting for transfers between devices  7.53 us (5%)
  between operations  6.85 us (5%)
  local copies, waits for them, and re-layouts  6.75 us (5%)
    ppermute x16, starting transfers between devices, passed_along(): return lax.ppermute(value, axis, pairs)  76.9 us
    all_to_all x1, blocking collectives, sent_and_summed(): lax.all_to_all(tiles, axis, split_axis=0, concat_axis=0, tiled=True)  12.6 us
    all_to_all x1, starting transfers between devices, sent_to_all(): return lax.all_to_all(copies, axis, split_axis=0, concat_axis=0, tiled=True)  10.2 us
    dot_general x9, matrix products, tile_terms(): first = jnp.dot(kern, panel_probes, preferred_element_type=jnp.float32)  7.25 us
    dot_general x9, matrix products, tile_terms(): second = jnp.dot(deriv, panel_probes, preferred_element_type=jnp.float32)  6.97 us
    all_to_all x1, starting transfers between devices, body(): lax.all_to_all(jnp.stack([features] * lax.axis_size('feat')), 'feat', 0, 0)  4.57 us
    ppermute x16, waiting for transfers between devices, passed_along(): return lax.ppermute(value, axis, pairs)  4.39 us
    gather x1, local copies, waits for them, and re-layouts, body(): ordered_all = jnp.take(all_probes, order[0], axis=0)  3.21 us
  transfers between devices with their start and end apart: 18, of which 2 were waited for; matrix products, arithmetic and copies ran while one was open for 12% of the time, Pallas kernels for 0%

profile of v1, /device:TPU:1, one launch (start us, length us, event | category | flops | bytes accessed | tf_op | source)
XLA Modules:
  0.0 142.9 jit_solution(7718021502665522646)
XLA Ops:
  0.6 1.3 broadcast_in_dim.13
  2.0 10.2 %all-to-all-start.1 = ((bf16[4,1024,8]{1,2,0:T(8,128)(2,1)}), bf16[4,1024,8]{1,2,0:T(8,128)(2,1)S(1)}, u32[]{:S(2)}, u32[]{:S(2)}) async-start(bf16[4,1024,8]{1,2,0:T(8,128)(2,1)} %broadcast_in_dim.13), calls=%async_computation.1 | async-start | bytes 131072 | tf_op jit(solution)/shard_map/all_to_all | solution.py:9
  12.3 3.1 %all-to-all-done.1 = bf16[4,1024,8]{1,2,0:T(8,128)(2,1)S(1)} async-done(((bf16[4,1024,8]{1,2,0:T(8,128)(2,1)}), bf16[4,1024,8]{1,2,0:T(8,128)(2,1)S(1)}, u32[]{:S(2)}, u32[]{:S(2)}) %all-to-all-start.1) | async-done | bytes 65568 | tf_op jit(solution)/shard_map/all_to_all | solution.py:9
  15.6 3.2 %gather_fusion = bf16[1024,32]{1,0:T(8,128)(2,1)S(1)} fusion(bf16[1024,32]{1,0:T(8,128)(2,1)S(1)} %copy.9, s32[1024]{0:T(1024)S(1)} %broadcast_clamp_fusion), kind=kCustom, calls=%fused_computation | custom fusion | bytes 135168 | tf_op jit(solution)/shard_map/jit(_take)/gather | solution.py:74
  19.0 1.9 %collective-permute-start.3 = (bf16[256,32]{1,0:T(8,128)(2,1)S(1)}, bf16[256,32]{1,0:T(8,128)(2,1)S(1)}, u32[]{:S(2)}, u32[]{:S(2)}) collective-permute-start(bf16[256,32]{1,0:T(8,128)(2,1)S(1)} %dynamic-slice_select_fusion), channel_id=1, source_target_pairs={{0,4},{4,8},{8,12},{12,16},{16,20},{20,24},{24,28},{28,32},{32,36}... | collective-permute-start | bytes 49160 | tf_op jit(solution)/shard_map/ppermute | solution.py:26
  20.9 10.7 %collective-permute-start.1 = (bf16[256,32]{1,0:T(8,128)(2,1)S(1)}, bf16[256,32]{1,0:T(8,128)(2,1)S(1)}, u32[]{:S(2)}, u32[]{:S(2)}) collective-permute-start(bf16[256,32]{1,0:T(8,128)(2,1)S(1)} %dynamic-slice_select_fusion), channel_id=1, source_target_pairs={{0,508},{4,0},{8,4},{12,8},{16,12},{20,16},{24,20},{28,24},{32,28}... | collective-permute-start | bytes 49160 | tf_op jit(solution)/shard_map/ppermute | solution.py:26
  32.2 4.6 %all-to-all-start = ((bf16[4,1024,16]{1,2,0:T(8,128)(2,1)}), bf16[4,1024,16]{1,2,0:T(8,128)(2,1)S(1)}, u32[]{:S(2)}, u32[]{:S(2)}) async-start(bf16[4,1024,16]{1,2,0:T(8,128)(2,1)} %stack.2), calls=%async_computation | async-start | bytes 262144 | tf_op jit(solution)/shard_map/all_to_all | solution.py:50
  36.8 1.9 %collective-permute-start.7 = (bf16[256,32]{1,0:T(8,128)(2,1)S(1)}, bf16[256,32]{1,0:T(8,128)(2,1)S(1)}, u32[]{:S(2)}, u32[]{:S(2)}) collective-permute-start(bf16[256,32]{1,0:T(8,128)(2,1)S(1)} %collective-permute-done.3), channel_id=1, source_target_pairs={{0,4},{4,8},{8,12},{12,16},{16,20},{20,24},{24,28},{28,32},{32,36}... | collective-permute-start | bytes 49160 | tf_op jit(solution)/shard_map/ppermute | solution.py:26
  38.7 9.1 %collective-permute-start.5 = (bf16[256,32]{1,0:T(8,128)(2,1)S(1)}, bf16[256,32]{1,0:T(8,128)(2,1)S(1)}, u32[]{:S(2)}, u32[]{:S(2)}) collective-permute-start(bf16[256,32]{1,0:T(8,128)(2,1)S(1)} %collective-permute-done.1), channel_id=1, source_target_pairs={{0,508},{4,0},{8,4},{12,8},{16,12},{20,16},{24,20},{28,24},{32,28}... | collective-permute-start | bytes 49160 | tf_op jit(solution)/shard_map/ppermute | solution.py:26
  54.2 1.9 %collective-permute-start.11 = (bf16[256,32]{1,0:T(8,128)(2,1)S(1)}, bf16[256,32]{1,0:T(8,128)(2,1)S(1)}, u32[]{:S(2)}, u32[]{:S(2)}) collective-permute-start(bf16[256,32]{1,0:T(8,128)(2,1)S(1)} %collective-permute-done.7), channel_id=1, source_target_pairs={{0,4},{4,8},{8,12},{12,16},{16,20},{20,24},{24,28},{28,32},{32,36}... | collective-permute-start | bytes 49160 | tf_op jit(solution)/shard_map/ppermute | solution.py:26
  56.1 9.1 %collective-permute-start.9 = (bf16[256,32]{1,0:T(8,128)(2,1)S(1)}, bf16[256,32]{1,0:T(8,128)(2,1)S(1)}, u32[]{:S(2)}, u32[]{:S(2)}) collective-permute-start(bf16[256,32]{1,0:T(8,128)(2,1)S(1)} %collective-permute-done.5), channel_id=1, source_target_pairs={{0,508},{4,0},{8,4},{12,8},{16,12},{20,16},{24,20},{28,24},{32,28}... | collective-permute-start | bytes 49160 | tf_op jit(solution)/shard_map/ppermute | solution.py:26
  65.3 1.9 %collective-permute-start = (bf16[256,64]{0,1:T(8,128)(2,1)S(1)}, bf16[256,64]{0,1:T(8,128)(2,1)S(1)}, u32[]{:S(2)}, u32[]{:S(2)}) collective-permute-start(bf16[256,64]{0,1:T(8,128)(2,1)S(1)} %get-tuple-element.3), channel_id=1, source_target_pairs={{0,508},{4,0},{8,4},{12,8},{16,12},{20,16},{24,20},{28,24},{32,28}... | collective-permute-start | bytes 98312 | tf_op jit(solution)/shard_map/ppermute | solution.py:26
  67.2 3.4 %collective-permute-start.2 = (bf16[256,64]{0,1:T(8,128)(2,1)S(1)}, bf16[256,64]{0,1:T(8,128)(2,1)S(1)}, u32[]{:S(2)}, u32[]{:S(2)}) collective-permute-start(bf16[256,64]{0,1:T(8,128)(2,1)S(1)} %get-tuple-element.3), channel_id=1, source_target_pairs={{0,4},{4,8},{8,12},{12,16},{16,20},{20,24},{24,28},{28,32},{32,36}... | collective-permute-start | bytes 98312 | tf_op jit(solution)/shard_map/ppermute | solution.py:26
  72.2 1.9 %collective-permute-start.15 = (bf16[256,32]{1,0:T(8,128)(2,1)S(1)}, bf16[256,32]{1,0:T(8,128)(2,1)S(1)}, u32[]{:S(2)}, u32[]{:S(2)}) collective-permute-start(bf16[256,32]{1,0:T(8,128)(2,1)S(1)} %collective-permute-done.11), channel_id=1, source_target_pairs={{0,4},{4,8},{8,12},{12,16},{16,20},{20,24},{24,28},{28,32},{32,36}... | collective-permute-start | bytes 49160 | tf_op jit(solution)/shard_map/ppermute | solution.py:26
  74.1 9.1 %collective-permute-start.13 = (bf16[256,32]{1,0:T(8,128)(2,1)S(1)}, bf16[256,32]{1,0:T(8,128)(2,1)S(1)}, u32[]{:S(2)}, u32[]{:S(2)}) collective-permute-start(bf16[256,32]{1,0:T(8,128)(2,1)S(1)} %collective-permute-done.9), channel_id=1, source_target_pairs={{0,508},{4,0},{8,4},{12,8},{16,12},{20,16},{24,20},{28,24},{32,28}... | collective-permute-start | bytes 49160 | tf_op jit(solution)/shard_map/ppermute | solution.py:26
  83.3 1.9 %collective-permute-start.4 = (bf16[256,64]{0,1:T(8,128)(2,1)S(1)}, bf16[256,64]{0,1:T(8,128)(2,1)S(1)}, u32[]{:S(2)}, u32[]{:S(2)}) collective-permute-start(bf16[256,64]{0,1:T(8,128)(2,1)S(1)} %collective-permute-done), channel_id=1, source_target_pairs={{0,508},{4,0},{8,4},{12,8},{16,12},{20,16},{24,20},{28,24},{32,28}... | collective-permute-start | bytes 98312 | tf_op jit(solution)/shard_map/ppermute | solution.py:26
  85.2 3.4 %collective-permute-start.6 = (bf16[256,64]{0,1:T(8,128)(2,1)S(1)}, bf16[256,64]{0,1:T(8,128)(2,1)S(1)}, u32[]{:S(2)}, u32[]{:S(2)}) collective-permute-start(bf16[256,64]{0,1:T(8,128)(2,1)S(1)} %collective-permute-done.2), channel_id=1, source_target_pairs={{0,4},{4,8},{8,12},{12,16},{16,20},{20,24},{24,28},{28,32},{32,36}... | collective-permute-start | bytes 98312 | tf_op jit(solution)/shard_map/ppermute | solution.py:26
  92.6 7.6 %collective-permute-start.8 = (bf16[256,64]{0,1:T(8,128)(2,1)S(1)}, bf16[256,64]{0,1:T(8,128)(2,1)S(1)}, u32[]{:S(2)}, u32[]{:S(2)}) collective-permute-start(bf16[256,64]{0,1:T(8,128)(2,1)S(1)} %collective-permute-done.4), channel_id=1, source_target_pairs={{0,508},{4,0},{8,4},{12,8},{16,12},{20,16},{24,20},{28,24},{32,28}... | collective-permute-start | bytes 98312 | tf_op jit(solution)/shard_map/ppermute | solution.py:26
  100.3 1.9 %collective-permute-start.10 = (bf16[256,64]{0,1:T(8,128)(2,1)S(1)}, bf16[256,64]{0,1:T(8,128)(2,1)S(1)}, u32[]{:S(2)}, u32[]{:S(2)}) collective-permute-start(bf16[256,64]{0,1:T(8,128)(2,1)S(1)} %collective-permute-done.6), channel_id=1, source_target_pairs={{0,4},{4,8},{8,12},{12,16},{16,20},{20,24},{24,28},{28,32},{32,36}... | collective-permute-start | bytes 98312 | tf_op jit(solution)/shard_map/ppermute | solution.py:26
  106.2 9.1 %collective-permute-start.12 = (bf16[256,64]{0,1:T(8,128)(2,1)S(1)}, bf16[256,64]{0,1:T(8,128)(2,1)S(1)}, u32[]{:S(2)}, u32[]{:S(2)}) collective-permute-start(bf16[256,64]{0,1:T(8,128)(2,1)S(1)} %collective-permute-done.8), channel_id=1, source_target_pairs={{0,508},{4,0},{8,4},{12,8},{16,12},{20,16},{24,20},{28,24},{32,28}... | collective-permute-start | bytes 98312 | tf_op jit(solution)/shard_map/ppermute | solution.py:26
  115.3 2.1 %collective-permute-start.14 = (bf16[256,64]{0,1:T(8,128)(2,1)S(1)}, bf16[256,64]{0,1:T(8,128)(2,1)S(1)}, u32[]{:S(2)}, u32[]{:S(2)}) collective-permute-start(bf16[256,64]{0,1:T(8,128)(2,1)S(1)} %collective-permute-done.10), channel_id=1, source_target_pairs={{0,4},{4,8},{8,12},{12,16},{16,20},{20,24},{24,28},{28,32},{32,36}... | collective-permute-start | bytes 98312 | tf_op jit(solution)/shard_map/ppermute | solution.py:26
  119.7 0.8 fusion.23
  121.3 4.3 %collective-permute-done.14 = bf16[256,64]{0,1:T(8,128)(2,1)S(1)} collective-permute-done((bf16[256,64]{0,1:T(8,128)(2,1)S(1)}, bf16[256,64]{0,1:T(8,128)(2,1)S(1)}, u32[]{:S(2)}, u32[]{:S(2)}) %collective-permute-start.14) | collective-permute-done | bytes 32800 | tf_op jit(solution)/shard_map/ppermute | solution.py:26
  129.7 12.6 %all_to_all.15 = f32[4,2048,8]{1,2,0:T(8,128)S(1)} all-to-all(f32[4,2048,8]{1,2,0:T(8,128)S(1)} %maximum_bitcast_fusion), channel_id=1, replica_groups=mesh['rows'=128,'feat'=4] {'feat'}, dimensions={0} | all-to-all | bytes 524288 | tf_op jit(solution)/shard_map/all_to_all | solution.py:37
  (69 shorter events, 18.9 us)
Async XLA Ops:
  2.0 10.2 %copy-start.2 = (s32[1,1024]{1,0:T(1,128)S(1)}, s32[1,1024]{1,0:T(1,128)}, u32[]{:S(2)}) copy-start(s32[1,1024]{1,0:T(1,128)} %param.9) | copy-start | bytes 12292
  2.0 13.5 %all-to-all-start.1 = ((bf16[4,1024,8]{1,2,0:T(8,128)(2,1)}), bf16[4,1024,8]{1,2,0:T(8,128)(2,1)S(1)}, u32[]{:S(2)}, u32[]{:S(2)}) async-start(bf16[4,1024,8]{1,2,0:T(8,128)(2,1)} %broadcast_in_dim.13), calls=%async_computation.1 | async-start | bytes 131072 | tf_op jit(solution)/shard_map/all_to_all | solution.py:9
  18.8 12.7 %copy-start = (bf16[1024,16]{0,1:T(8,128)(2,1)S(1)}, bf16[1024,16]{0,1:T(8,128)(2,1)}, u32[]{:S(2)}) copy-start(bf16[1024,16]{0,1:T(8,128)(2,1)} %param.5) | copy-start | bytes 98308
  19.0 17.9 %collective-permute-start.3 = (bf16[256,32]{1,0:T(8,128)(2,1)S(1)}, bf16[256,32]{1,0:T(8,128)(2,1)S(1)}, u32[]{:S(2)}, u32[]{:S(2)}) collective-permute-start(bf16[256,32]{1,0:T(8,128)(2,1)S(1)} %dynamic-slice_select_fusion), channel_id=1, source_target_pairs={{0,4},{4,8},{8,12},{12,16},{16,20},{20,24},{24,28},{28,32},{32,36}... | collective-permute-start | bytes 49160 | tf_op jit(solution)/shard_map/ppermute | solution.py:26
  20.9 17.8 %collective-permute-start.1 = (bf16[256,32]{1,0:T(8,128)(2,1)S(1)}, bf16[256,32]{1,0:T(8,128)(2,1)S(1)}, u32[]{:S(2)}, u32[]{:S(2)}) collective-permute-start(bf16[256,32]{1,0:T(8,128)(2,1)S(1)} %dynamic-slice_select_fusion), channel_id=1, source_target_pairs={{0,508},{4,0},{8,4},{12,8},{16,12},{20,16},{24,20},{28,24},{32,28}... | collective-permute-start | bytes 49160 | tf_op jit(solution)/shard_map/ppermute | solution.py:26
  32.2 15.6 %copy-start.1 = (s32[1,9]{1,0:T(1,128)S(1)}, s32[1,9]{1,0:T(1,128)}, u32[]{:S(2)}) copy-start(s32[1,9]{1,0:T(1,128)} %param.8) | copy-start | bytes 112
  32.2 33.0 %all-to-all-start = ((bf16[4,1024,16]{1,2,0:T(8,128)(2,1)}), bf16[4,1024,16]{1,2,0:T(8,128)(2,1)S(1)}, u32[]{:S(2)}, u32[]{:S(2)}) async-start(bf16[4,1024,16]{1,2,0:T(8,128)(2,1)} %stack.2), calls=%async_computation | async-start | bytes 262144 | tf_op jit(solution)/shard_map/all_to_all | solution.py:50
  36.8 17.4 %collective-permute-start.7 = (bf16[256,32]{1,0:T(8,128)(2,1)S(1)}, bf16[256,32]{1,0:T(8,128)(2,1)S(1)}, u32[]{:S(2)}, u32[]{:S(2)}) collective-permute-start(bf16[256,32]{1,0:T(8,128)(2,1)S(1)} %collective-permute-done.3), channel_id=1, source_target_pairs={{0,4},{4,8},{8,12},{12,16},{16,20},{20,24},{24,28},{28,32},{32,36}... | collective-permute-start | bytes 49160 | tf_op jit(solution)/shard_map/ppermute | solution.py:26
  38.7 17.4 %collective-permute-start.5 = (bf16[256,32]{1,0:T(8,128)(2,1)S(1)}, bf16[256,32]{1,0:T(8,128)(2,1)S(1)}, u32[]{:S(2)}, u32[]{:S(2)}) collective-permute-start(bf16[256,32]{1,0:T(8,128)(2,1)S(1)} %collective-permute-done.1), channel_id=1, source_target_pairs={{0,508},{4,0},{8,4},{12,8},{16,12},{20,16},{24,20},{28,24},{32,28}... | collective-permute-start | bytes 49160 | tf_op jit(solution)/shard_map/ppermute | solution.py:26
  54.2 18.0 %collective-permute-start.11 = (bf16[256,32]{1,0:T(8,128)(2,1)S(1)}, bf16[256,32]{1,0:T(8,128)(2,1)S(1)}, u32[]{:S(2)}, u32[]{:S(2)}) collective-permute-start(bf16[256,32]{1,0:T(8,128)(2,1)S(1)} %collective-permute-done.7), channel_id=1, source_target_pairs={{0,4},{4,8},{8,12},{12,16},{16,20},{20,24},{24,28},{28,32},{32,36}... | collective-permute-start | bytes 49160 | tf_op jit(solution)/shard_map/ppermute | solution.py:26
  56.1 18.0 %collective-permute-start.9 = (bf16[256,32]{1,0:T(8,128)(2,1)S(1)}, bf16[256,32]{1,0:T(8,128)(2,1)S(1)}, u32[]{:S(2)}, u32[]{:S(2)}) collective-permute-start(bf16[256,32]{1,0:T(8,128)(2,1)S(1)} %collective-permute-done.5), channel_id=1, source_target_pairs={{0,508},{4,0},{8,4},{12,8},{16,12},{20,16},{24,20},{28,24},{32,28}... | collective-permute-start | bytes 49160 | tf_op jit(solution)/shard_map/ppermute | solution.py:26
  65.3 18.0 %collective-permute-start = (bf16[256,64]{0,1:T(8,128)(2,1)S(1)}, bf16[256,64]{0,1:T(8,128)(2,1)S(1)}, u32[]{:S(2)}, u32[]{:S(2)}) collective-permute-start(bf16[256,64]{0,1:T(8,128)(2,1)S(1)} %get-tuple-element.3), channel_id=1, source_target_pairs={{0,508},{4,0},{8,4},{12,8},{16,12},{20,16},{24,20},{28,24},{32,28}... | collective-permute-start | bytes 98312 | tf_op jit(solution)/shard_map/ppermute | solution.py:26
  67.2 18.0 %collective-permute-start.2 = (bf16[256,64]{0,1:T(8,128)(2,1)S(1)}, bf16[256,64]{0,1:T(8,128)(2,1)S(1)}, u32[]{:S(2)}, u32[]{:S(2)}) collective-permute-start(bf16[256,64]{0,1:T(8,128)(2,1)S(1)} %get-tuple-element.3), channel_id=1, source_target_pairs={{0,4},{4,8},{8,12},{12,16},{16,20},{20,24},{24,28},{28,32},{32,36}... | collective-permute-start | bytes 98312 | tf_op jit(solution)/shard_map/ppermute | solution.py:26
  72.2 53.8 %collective-permute-start.15 = (bf16[256,32]{1,0:T(8,128)(2,1)S(1)}, bf16[256,32]{1,0:T(8,128)(2,1)S(1)}, u32[]{:S(2)}, u32[]{:S(2)}) collective-permute-start(bf16[256,32]{1,0:T(8,128)(2,1)S(1)} %collective-permute-done.11), channel_id=1, source_target_pairs={{0,4},{4,8},{8,12},{12,16},{16,20},{20,24},{24,28},{28,32},{32,36}... | collective-permute-start | bytes 49160 | tf_op jit(solution)/shard_map/ppermute | solution.py:26
  74.1 53.9 %collective-permute-start.13 = (bf16[256,32]{1,0:T(8,128)(2,1)S(1)}, bf16[256,32]{1,0:T(8,128)(2,1)S(1)}, u32[]{:S(2)}, u32[]{:S(2)}) collective-permute-start(bf16[256,32]{1,0:T(8,128)(2,1)S(1)} %collective-permute-done.9), channel_id=1, source_target_pairs={{0,508},{4,0},{8,4},{12,8},{16,12},{20,16},{24,20},{28,24},{32,28}... | collective-permute-start | bytes 49160 | tf_op jit(solution)/shard_map/ppermute | solution.py:26
  83.3 9.3 %collective-permute-start.4 = (bf16[256,64]{0,1:T(8,128)(2,1)S(1)}, bf16[256,64]{0,1:T(8,128)(2,1)S(1)}, u32[]{:S(2)}, u32[]{:S(2)}) collective-permute-start(bf16[256,64]{0,1:T(8,128)(2,1)S(1)} %collective-permute-done), channel_id=1, source_target_pairs={{0,508},{4,0},{8,4},{12,8},{16,12},{20,16},{24,20},{28,24},{32,28}... | collective-permute-start | bytes 98312 | tf_op jit(solution)/shard_map/ppermute | solution.py:26
  85.2 15.0 %collective-permute-start.6 = (bf16[256,64]{0,1:T(8,128)(2,1)S(1)}, bf16[256,64]{0,1:T(8,128)(2,1)S(1)}, u32[]{:S(2)}, u32[]{:S(2)}) collective-permute-start(bf16[256,64]{0,1:T(8,128)(2,1)S(1)} %collective-permute-done.2), channel_id=1, source_target_pairs={{0,4},{4,8},{8,12},{12,16},{16,20},{20,24},{24,28},{28,32},{32,36}... | collective-permute-start | bytes 98312 | tf_op jit(solution)/shard_map/ppermute | solution.py:26
  92.6 13.5 %collective-permute-start.8 = (bf16[256,64]{0,1:T(8,128)(2,1)S(1)}, bf16[256,64]{0,1:T(8,128)(2,1)S(1)}, u32[]{:S(2)}, u32[]{:S(2)}) collective-permute-start(bf16[256,64]{0,1:T(8,128)(2,1)S(1)} %collective-permute-done.4), channel_id=1, source_target_pairs={{0,508},{4,0},{8,4},{12,8},{16,12},{20,16},{24,20},{28,24},{32,28}... | collective-permute-start | bytes 98312 | tf_op jit(solution)/shard_map/ppermute | solution.py:26
  100.3 15.0 %collective-permute-start.10 = (bf16[256,64]{0,1:T(8,128)(2,1)S(1)}, bf16[256,64]{0,1:T(8,128)(2,1)S(1)}, u32[]{:S(2)}, u32[]{:S(2)}) collective-permute-start(bf16[256,64]{0,1:T(8,128)(2,1)S(1)} %collective-permute-done.6), channel_id=1, source_target_pairs={{0,4},{4,8},{8,12},{12,16},{16,20},{20,24},{24,28},{28,32},{32,36}... | collective-permute-start | bytes 98312 | tf_op jit(solution)/shard_map/ppermute | solution.py:26
  106.2 21.5 %collective-permute-start.12 = (bf16[256,64]{0,1:T(8,128)(2,1)S(1)}, bf16[256,64]{0,1:T(8,128)(2,1)S(1)}, u32[]{:S(2)}, u32[]{:S(2)}) collective-permute-start(bf16[256,64]{0,1:T(8,128)(2,1)S(1)} %collective-permute-done.8), channel_id=1, source_target_pairs={{0,508},{4,0},{8,4},{12,8},{16,12},{20,16},{24,20},{28,24},{32,28}... | collective-permute-start | bytes 98312 | tf_op jit(solution)/shard_map/ppermute | solution.py:26
  115.3 10.4 %collective-permute-start.14 = (bf16[256,64]{0,1:T(8,128)(2,1)S(1)}, bf16[256,64]{0,1:T(8,128)(2,1)S(1)}, u32[]{:S(2)}, u32[]{:S(2)}) collective-permute-start(bf16[256,64]{0,1:T(8,128)(2,1)S(1)} %collective-permute-done.10), channel_id=1, source_target_pairs={{0,4},{4,8},{8,12},{12,16},{16,20},{20,24},{24,28},{28,32},{32,36}... | collective-permute-start | bytes 98312 | tf_op jit(solution)/shard_map/ppermute | solution.py:26
